TPU v7x, 32 devices: a whole 2x2x4 slice. The times are simulated.
32 devices in a mesh: shard: 8 (over z, x), width: 4 (over y, core).
Axes of the slice: x: 2, y: 2, z: 4, core: 2. Of those that a mesh axis runs over, the one named last changes fastest.
Arguments:
- w_gate: bfloat16 [2048, 8192], P('shard', 'width'), may hold values from -0.125 to 0.125
- low_gate: bfloat16 [2048, 64], P('shard'), may hold values from -0.125 to 0.125
- high_gate: bfloat16 [64, 8192], P(None, 'width'), may hold values from -0.75 to 0.75
- w_up: bfloat16 [2048, 8192], P('shard', 'width'), may hold values from -0.125 to 0.125
- low_up: bfloat16 [2048, 64], P('shard'), may hold values from -0.125 to 0.125
- high_up: bfloat16 [64, 8192], P(None, 'width'), may hold values from -0.75 to 0.75
- w_down: bfloat16 [8192, 2048], P('width', 'shard'), may hold values from -0.0625 to 0.0625
- low_down: bfloat16 [8192, 64], P('width'), may hold values from -0.0625 to 0.0625
- high_down: bfloat16 [64, 2048], P(None, 'shard'), may hold values from -0.75 to 0.75
- norm_train: float32 [2048], P(('shard', 'width')), may hold values from 0.25 to 1.75
- norm_step: float32 [2048], P(('shard', 'width')), may hold values from -0.3 to 0.3
Outputs:
- serve_gate: bfloat16 [8192, 2048], P('width')
- serve_up: bfloat16 [8192, 2048], P('width')
- serve_down: bfloat16 [2048, 8192], P(None, 'width')
- serve_norm: bfloat16 [2048], replicated
All inputs are finite; a program needn't handle non-finite values.
Results may differ from a plain program's by a relative error of at most 0.001.
Values may be sent and summed in bfloat16 or wider, within the bound.
A program may use at most 128 MiB of HBM per device.

v0:
```python
import jax
import jax.numpy as jnp
from jax import lax
from jax.sharding import PartitionSpec as P

mix_rate = 2.0


def body(
    w_gate,
    low_gate,
    high_gate,
    w_up,
    low_up,
    high_up,
    w_down,
    low_down,
    high_down,
    norm_train,
    norm_step,
):
    fresh_gate = w_gate.astype(jnp.float32) + mix_rate * jnp.dot(
        low_gate, high_gate, preferred_element_type=jnp.float32
    )
    fresh_up = w_up.astype(jnp.float32) + mix_rate * jnp.dot(
        low_up, high_up, preferred_element_type=jnp.float32
    )
    fresh_down = w_down.astype(jnp.float32) + mix_rate * jnp.dot(
        low_down, high_down, preferred_element_type=jnp.float32
    )
    narrow_gate, narrow_up, narrow_down = (
        fresh_gate.astype(jnp.bfloat16),
        fresh_up.astype(jnp.bfloat16),
        fresh_down.astype(jnp.bfloat16),
    )
    serve_gate, serve_up, serve_down = (
        lax.all_gather(narrow_gate, "shard", axis=0, tiled=True),
        lax.all_gather(narrow_up, "shard", axis=0, tiled=True),
        lax.all_gather(narrow_down, "shard", axis=1, tiled=True),
    )
    serve_gate, serve_up, serve_down = (serve_gate.T, serve_up.T, serve_down.T)
    serve_norm = lax.all_gather(
        (norm_train + norm_step).astype(jnp.bfloat16), ("shard", "width"), axis=0, tiled=True
    )
    return (serve_gate, serve_up, serve_down, serve_norm)


def solution(mesh):
    return jax.shard_map(
        body,
        mesh=mesh,
        in_specs=(
            P("shard", "width"),
            P("shard", None),
            P(None, "width"),
            P("shard", "width"),
            P("shard", None),
            P(None, "width"),
            P("width", "shard"),
            P("width", None),
            P(None, "shard"),
            P(("shard", "width")),
            P(("shard", "width")),
        ),
        out_specs=(P("width", None), P("width", None), P(None, "width"), P()),
        check_vma=False,
    )
```

profile of v0, /device:TPU:0, one launch (start us, length us, event | category | flops | bytes accessed | tf_op | source)
XLA Modules:
  0.0 408.6 jit_solution(10332017895231233295)
XLA Ops:
  7.2 0.0 copy-start
  7.2 0.0 copy-start.1
  7.2 0.0 copy-start.5
  7.2 0.0 copy-start.3
  7.2 0.0 all-gather.4.cloned.1.call-start
  7.3 0.9 copy-done
  8.1 2.7 fusion.3
  10.8 0.0 copy-start.2
  10.8 0.0 copy-start.4
  10.8 0.0 copy-start.6
  10.8 0.0 all-gather.4.cloned.1.call-update
  10.8 0.0 all-gather.6.cloned.1.call-start
  10.9 0.0 copy-done.1
  10.9 0.0 copy-done.5
  10.9 0.0 copy-done.3
  10.9 1.4 fusion.4
  12.3 0.0 copy-start.7
  12.3 0.0 copy-start.8
  12.3 0.0 all-gather.6.cloned.1.call-update
  12.4 0.0 all-gather.8.cloned.1.call-start
  12.4 0.0 copy-done.2
  12.4 0.0 copy-done.4
  12.4 0.0 copy-done.6
  12.4 1.5 fusion.5
  14.0 0.0 all-gather.8.cloned.1.call-update
  14.0 0.0 copy-done.7
  14.0 0.0 copy-done.8
  14.1 0.2 dynamic-update-slice
  14.3 45.8 %all-reduce = bf16[2048]{0:T(1024)(128)(2,1)} all-reduce(bf16[2048]{0:T(1024)(128)(2,1)S(1)} %dynamic-update-slice), channel_id=1, replica_groups=mesh['shard'=8,'width'=4] {'shard','width'}, use_global_device_ids=true, to_apply=%add | all-reduce | flops 2048 | bytes 8192
  60.2 79.1 %all-gather.4.cloned.1.call-done = bf16[2048,2048]{1,0:T(8,128)(2,1)} async-done(((bf16[256,2048]{1,0:T(8,128)(2,1)}), bf16[2048,2048]{1,0:T(8,128)(2,1)}) %all-gather.4.cloned.1.call-update) | async-done | bytes 8388624 | tf_op jit(solution)/shard_map/all_gather | solution.py:37
  139.2 12.3 %copy.15 = bf16[2048,2048]{1,0:T(8,128)(2,1)} copy(bf16[2048,2048]{0,1:T(8,128)(2,1)} %bitcast.9) | data formatting | bytes 16777216
  151.6 113.0 %all-gather.6.cloned.1.call-done = bf16[2048,2048]{1,0:T(8,128)(2,1)} async-done(((bf16[256,2048]{1,0:T(8,128)(2,1)}), bf16[2048,2048]{1,0:T(8,128)(2,1)}) %all-gather.6.cloned.1.call-update) | async-done | bytes 8388624 | tf_op jit(solution)/shard_map/all_gather | solution.py:38
  264.6 12.3 %copy.16 = bf16[2048,2048]{1,0:T(8,128)(2,1)} copy(bf16[2048,2048]{0,1:T(8,128)(2,1)} %bitcast.10) | data formatting | bytes 16777216
  277.0 112.9 %all-gather.8.cloned.1.call-done = bf16[2048,2048]{1,0:T(8,128)(2,1)} async-done(((bf16[2048,256]{1,0:T(8,128)(2,1)}), bf16[2048,2048]{1,0:T(8,128)(2,1)}) %all-gather.8.cloned.1.call-update) | async-done | bytes 8388624 | tf_op jit(solution)/shard_map/all_gather | solution.py:39
  389.8 12.2 %copy.17 = bf16[2048,2048]{1,0:T(8,128)(2,1)} copy(bf16[2048,2048]{0,1:T(8,128)(2,1)} %bitcast.11) | data formatting | bytes 16777216
  (2 shorter events, 0.0 us)
Async XLA Ops:
  7.2 1.0 copy-start
  7.2 3.7 copy-start.1
  7.2 3.7 copy-start.5
  7.2 3.7 copy-start.3
  7.2 132.0 %all-gather.4.cloned.1.call-start = ((), (), s32[]{:S(2)}) async-start(), calls=%async_computation | async-start | bytes 9437184 | tf_op jit(solution)/shard_map/all_gather | solution.py:37
  10.8 1.6 copy-start.2
  10.8 1.6 copy-start.4
  10.8 1.6 copy-start.6
  10.8 253.8 %all-gather.6.cloned.1.call-start = ((), (), s32[]{:S(2)}) async-start(), calls=%async_computation.1 | async-start | bytes 9437184 | tf_op jit(solution)/shard_map/all_gather | solution.py:38
  12.3 1.7 copy-start.7
  12.3 1.7 copy-start.8
  12.4 377.4 %all-gather.8.cloned.1.call-start = ((), (), s32[]{:S(2)}) async-start(), calls=%async_computation.2 | async-start | bytes 9437184 | tf_op jit(solution)/shard_map/all_gather | solution.py:39
Sparse Core Ops, SparseCore 0:
  10.9 128.2 all-gather.3
  141.9 122.6 all-gather.5
  266.7 123.1 all-gather.7
where the time goes:
time: 410 us; the launch traced here: 409 us
  waiting for transfers between devices  305 us (74%)
  blocking collectives  45.8 us (11%)
  local copies, waits for them, and re-layouts  38.1 us (9%)
  between operations  13.9 us (3%)
  matrix products  5.64 us (1%)
    all_gather x1, waiting for transfers between devices, body(): lax.all_gather(narrow_up, 'shard', axis=0, tiled=True)  113 us
    all_gather x1, waiting for transfers between devices, body(): lax.all_gather(narrow_down, 'shard', axis=1, tiled=True)  113 us
    all_gather x1, waiting for transfers between devices, body(): lax.all_gather(narrow_gate, 'shard', axis=0, tiled=True)  79.1 us
    unnamed x1, blocking collectives  45.8 us
    unnamed x23, local copies, waits for them, and re-layouts  38.1 us
  transfers between devices with their start and end apart: 3, of which 3 were waited for; matrix products, arithmetic and copies ran while one was open for 7% of the time, Pallas kernels for 0%

commit v1 on v0

v1 whole, which is shorter than its diff:
```python
import functools

import jax
import jax.numpy as jnp
from jax import lax
from jax.experimental import pallas as pl
from jax.experimental.pallas import tpu as pltpu
from jax.sharding import PartitionSpec as P

mix_rate = 2.0
MESH = pl.DeviceIdType.MESH
X = 2


def merged(w, low, high):
    fresh = w.astype(jnp.float32) + mix_rate * jnp.dot(
        low, high, preferred_element_type=jnp.float32
    )
    return fresh.astype(jnp.bfloat16)


PIECES = ((0, 0), (1, 0), (2, 0), (0, 1), (1, 1), (2, 1))
LINE = tuple(range(len(PIECES) - 1))
PAIR = len(PIECES) - 1
UP, DOWN, SIDE = 0, 1, 2


def gather_kernel(
    shards, widths, gate, up, down, norm, o_gate, o_up, o_down, o_norm,
    send_sem, recv_sem, norm_send, norm_recv, own_sem,
):
    lines = shards // X
    me, w = lax.axis_index("shard"), lax.axis_index("width")
    z, x = me // X, me % X
    partner = z * X + (1 - x)
    blocks, outs = (gate, up, down), (o_gate, o_up, o_down)
    n_pieces = len(PIECES)

    def own(c):
        t, h = PIECES[c]
        ref = blocks[t]
        if t < 2:
            half = ref.shape[0] // 2
            return ref.at[pl.ds(h * half, half), :]
        half = ref.shape[1] // 2
        return ref.at[:, pl.ds(h * half, half)]

    def place(s, c):
        t, h = PIECES[c]
        ref, out = blocks[t], outs[t]
        if t < 2:
            half, wide = ref.shape[0] // 2, ref.shape[1]
            return out.at[pl.ds(h * half, half), pl.ds(pl.multiple_of(s * wide, wide), wide)]
        half, tall = ref.shape[1] // 2, ref.shape[0]
        return out.at[pl.ds(pl.multiple_of(s * tall, tall), tall), pl.ds(h * half, half)]

    def target(way):
        return {UP: me + X, DOWN: me - X, SIDE: partner}[way]

    sends = []

    def when(conds, fn):
        if conds is None:
            fn()
        else:
            pl.when(conds)(fn)

    def has(way):
        return {UP: z + 1 < lines, DOWN: z > 0, SIDE: None}[way]

    def both(a, b):
        if a is None:
            return b
        if b is None:
            return a
        return jnp.logical_and(a, b)

    def send(way, s, c, slot, cond, from_own=False):
        def make():
            return pltpu.make_async_remote_copy(
                src_ref=own(c) if from_own else place(s, c),
                dst_ref=place(s, c),
                send_sem=send_sem.at[way, slot],
                recv_sem=recv_sem.at[s * n_pieces + c],
                device_id=(target(way), w),
                device_id_type=MESH,
            )

        full = both(cond, has(way))
        when(full, lambda: make().start())
        sends.append((full, lambda: make().wait_send()))

    def arrive(s, c, cond=None):
        when(
            cond,
            lambda: pltpu.make_async_remote_copy(
                src_ref=place(s, c),
                dst_ref=place(s, c),
                send_sem=send_sem.at[0, 0],
                recv_sem=recv_sem.at[s * n_pieces + c],
                device_id=(partner, w),
                device_id_type=MESH,
            ).wait_recv(),
        )

    def norm_rows(first, count):
        return o_norm.at[pl.ds(first, count)]

    def norm_copy(src, first, count, sem, rsem, dev):
        return pltpu.make_async_remote_copy(
            src_ref=src, dst_ref=norm_rows(first, count), send_sem=norm_send.at[sem],
            recv_sem=norm_recv.at[rsem], device_id=dev, device_id_type=MESH,
        )

    barrier = pltpu.get_barrier_semaphore()
    peers = [lax.rem(w + k, widths) for k in range(1, widths)]
    for p in peers:
        pl.semaphore_signal(barrier, inc=1, device_id=(me, p), device_id_type=MESH)
    for way in (UP, DOWN, SIDE):
        when(
            has(way),
            lambda way=way: pl.semaphore_signal(
                barrier, inc=1, device_id=(target(way), w), device_id_type=MESH
            ),
        )
    inner = jnp.logical_and(z > 0, z + 1 < lines)
    pl.when(inner)(lambda: pl.semaphore_wait(barrier, widths + 2))
    ends = widths + (1 if lines > 1 else 0)
    pl.when(jnp.logical_not(inner))(lambda: pl.semaphore_wait(barrier, ends))

    send(SIDE, me, PAIR, PAIR, None, from_own=True)
    for c in LINE:
        send(UP, me, c, c, None, from_own=True)
        send(DOWN, me, c, c, None, from_own=True)
        send(SIDE, me, c, c, None, from_own=True)
    kept = [pltpu.make_async_copy(own(c), place(me, c), own_sem.at[c]) for c in range(n_pieces)]
    norm_own = pltpu.make_async_copy(norm, norm_rows(me * widths + w, 1), own_sem.at[n_pieces])
    for copy in kept:
        copy.start()
    norm_own.start()
    tile_of = lambda k: norm_copy(norm, me * widths + w, 1, k - 1, k - 1, (me, peers[k - 1]))
    for k in range(1, widths):
        tile_of(k).start()
    norm_own.wait()
    for k in range(1, widths):
        source = lax.rem(w + widths - k, widths)
        norm_copy(norm, me * widths + source, 1, k - 1, k - 1, (me, peers[k - 1])).wait_recv()
    side_at = widths - 1
    norm_side = lambda s: norm_copy(
        norm_rows(s * widths, widths), s * widths, widths, side_at, side_at, (partner, w)
    )
    norm_side(me).start()

    for d in range(1, lines):
        for c in LINE:
            for way, s, cond in (
                (UP, me - d * X, z >= d),
                (DOWN, me + d * X, z + d < lines),
            ):
                arrive(s, c, cond)
                slot = d * n_pieces + c
                send(way, s, c, slot, cond)
                send(SIDE, s, c, slot + (way * lines * n_pieces), cond)

    arrive(partner, PAIR)
    norm_side(partner).wait_recv()

    def norm_pair(way, plane):
        rows = X * widths
        at = widths + way * lines
        return norm_copy(
            norm_rows(plane * rows, rows), plane * rows, rows,
            at + (plane - z) * (1 - 2 * way) * -1, widths + plane, (target(way), w),
        )

    line_slot = 2 * lines * n_pieces
    for d in range(lines):
        for way, plane, cond in (
            (UP, z - d, z >= d),
            (DOWN, z + d, z + d < lines),
        ):
            if d == 0:
                cond = None
            for j in range(X):
                s = me if (d == 0 and j == 0) else (partner if d == 0 else plane * X + j)
                if d > 0:
                    arrive(s, PAIR, cond)
                send(way, s, PAIR, line_slot + d * X + j, cond, from_own=(d == 0 and j == 0))
            full = both(cond, has(way))
            if d > 0:
                when(cond, lambda way=way, plane=plane: norm_pair(way, plane).wait_recv())
            when(full, lambda way=way, plane=plane: norm_pair(way, plane).start())
            sends.append((full, lambda way=way, plane=plane: norm_pair(way, plane).wait_send()))

    for c in LINE:
        arrive(partner, c)
    for d in range(1, lines):
        for c in LINE:
            arrive(partner - d * X, c, z >= d)
            arrive(partner + d * X, c, z + d < lines)
    for copy in kept:
        copy.wait()
    for k in range(1, widths):
        tile_of(k).wait_send()
    norm_side(me).wait_send()
    for cond, wait in sends:
        when(cond, wait)


def gather_all(shards, widths, gate, up, down, norm):
    lines = shards // X
    n_pieces = len(PIECES)
    any_ = pl.BlockSpec(memory_space=pl.ANY)
    vmem = pl.BlockSpec(memory_space=pltpu.VMEM)
    wide = lambda b: jax.ShapeDtypeStruct((b.shape[0], shards * b.shape[1]), b.dtype)
    tall = lambda b: jax.ShapeDtypeStruct((shards * b.shape[0], b.shape[1]), b.dtype)
    return pl.pallas_call(
        functools.partial(gather_kernel, shards, widths),
        out_shape=(
            wide(gate), wide(up), tall(down),
            jax.ShapeDtypeStruct((shards * widths,) + norm.shape[1:], norm.dtype),
        ),
        in_specs=[vmem] * 4,
        out_specs=(any_,) * 4,
        scratch_shapes=[
            pltpu.SemaphoreType.DMA((3, 2 * lines * n_pieces + lines * X)),
            pltpu.SemaphoreType.DMA((shards * n_pieces,)),
            pltpu.SemaphoreType.DMA((widths + 2 * lines,)),
            pltpu.SemaphoreType.DMA((widths + lines,)),
            pltpu.SemaphoreType.DMA((n_pieces + 1,)),
        ],
        compiler_params=pltpu.CompilerParams(collective_id=0, has_side_effects=True),
    )(gate, up, down, norm)


def body(
    shards,
    widths,
    w_gate,
    low_gate,
    high_gate,
    w_up,
    low_up,
    high_up,
    w_down,
    low_down,
    high_down,
    norm_train,
    norm_step,
):
    gate = merged(w_gate, low_gate, high_gate)
    up = merged(w_up, low_up, high_up)
    down = merged(w_down, low_down, high_down)
    gain = norm_train + norm_step
    if shards % X or gate.shape[0] % 128 or down.shape[0] % 256 or gain.shape[0] > 128:
        gate, up, down = (
            lax.all_gather(gate, "shard", axis=0, tiled=True),
            lax.all_gather(up, "shard", axis=0, tiled=True),
            lax.all_gather(down, "shard", axis=1, tiled=True),
        )
        gain = lax.all_gather(gain.astype(jnp.bfloat16), ("shard", "width"), axis=0, tiled=True)
        return gate.T, up.T, down.T, gain
    count = gain.shape[0]
    tile = jnp.pad(gain.reshape(1, 1, count), ((0, 0), (0, 7), (0, 128 - count)))
    gate, up, down, tiles = gather_all(shards, widths, gate.T, up.T, down.T, tile)
    return gate, up, down, tiles[:, 0, :count].reshape(-1).astype(jnp.bfloat16)


def solution(mesh):
    return jax.shard_map(
        functools.partial(body, mesh.shape["shard"], mesh.shape["width"]),
        mesh=mesh,
        in_specs=(
            P("shard", "width"),
            P("shard", None),
            P(None, "width"),
            P("shard", "width"),
            P("shard", None),
            P(None, "width"),
            P("width", "shard"),
            P("width", None),
            P(None, "shard"),
            P(("shard", "width")),
            P(("shard", "width")),
        ),
        out_specs=(P("width", None), P("width", None), P(None, "width"), P()),
        check_vma=False,
    )
```

time: 410 us -> 287 us (0.70)
  waiting for transfers between devices: 305 us -> 0 us
  Pallas kernels: 0 us -> 250 us
  blocking collectives: 45.8 us -> 0 us
  between operations: 13.9 us -> 0.73 us
  local copies, waits for them, and re-layouts: 38.1 us -> 30.6 us
    all_gather x3 -> x0, waiting for transfers between devices: 305 us -> none  [the longest x1 113 us: body(): lax.all_gather(narrow_up, 'shard', axis=0, tiled=True)]
    pallas_call x0 -> x1, Pallas kernels: none -> 250 us  [gather_all(): pl.pallas_call(functools.partial(gather_kernel, shards, widths), out_shap...]
    unnamed x1 -> x0, blocking collectives: 45.8 us -> none
    unnamed x23 -> x20, local copies, waits for them, and re-layouts: 38.1 us -> 28.4 us
  transfers between devices with their start and end apart: 3 -> 0, of which waited for: 3 -> 0; matrix products, arithmetic and copies ran while one was open for 7% -> 0% of each run, Pallas kernels for 0% -> 0%
where the time goes in v1:
time: 287 us
  Pallas kernels  250 us (87%)
  local copies, waits for them, and re-layouts  30.6 us (11%)
  matrix products  5.34 us (2%)
    pallas_call x1, Pallas kernels, gather_all(): pl.pallas_call(functools.partial(gather_kernel, shards, widths), out_shap...  250 us
    unnamed x20, local copies, waits for them, and re-layouts  28.4 us

profile of v1, /device:TPU:0, one launch (start us, length us, event | category | flops | bytes accessed | tf_op | source)
XLA Modules:
  0.0 287.2 jit_solution(15067906625950339638)
XLA Ops:
  0.6 0.0 copy-start
  0.6 0.0 copy-start.4
  0.7 0.7 add_bitcast_fusion
  1.4 0.6 pad.4.norm
  2.0 0.0 copy-start.1
  2.0 1.6 copy.21
  3.5 0.0 copy-done
  3.6 0.0 copy-done.4
  3.6 0.0 copy-start.5
  3.6 1.5 fusion.8.gate
  5.0 0.0 copy-done.1
  5.1 0.0 copy-start.2
  5.1 0.5 copy.23
  5.6 0.0 copy-done.5
  5.6 0.0 copy-start.6
  5.6 2.4 fusion.7.up
  8.0 0.0 copy-done.2
  8.0 0.0 copy-start.3
  8.0 0.6 copy.25
  8.7 0.0 copy-done.6
  8.7 0.3 copy-done.3
  9.0 1.4 fusion.6.down
  10.4 249.8 %shard_map.138 = (bf16[2048,2048]{1,0:T(8,128)(2,1)}, bf16[2048,2048]{1,0:T(8,128)(2,1)}, bf16[2048,2048]{1,0:T(8,128)(2,1)}, f32[32,8,128]{2,1,0:T(8,128)}) custom-call(bf16[2048,256]{1,0:T(8,128)(2,1)} %fusion.8.gate, bf16[2048,256]{1,0:T(8,128)(2,1)} %fusion.7.up, bf16[256,2048]{1,0:T(8,128)(2,1)} %fusion.6.down, f32[1,8,128]{2,1,0:T(8,128)} %pad.4.norm), custom_call_target="tpu_custom_call" | custom-call | tf_op jit(solution)/shard_map/pallas_call | solution.py:217
  260.2 1.0 fusion.9
  261.2 0.7 convert_element_type.30
  261.8 8.4 %copy.33 = bf16[2048,2048]{1,0:T(8,128)(2,1)} copy(bf16[2048,2048]{1,0:T(8,128)(2,1)} %get-tuple-element.16) | data formatting | bytes 16777216
  270.3 8.4 %copy.34 = bf16[2048,2048]{1,0:T(8,128)(2,1)} copy(bf16[2048,2048]{1,0:T(8,128)(2,1)} %get-tuple-element.17) | data formatting | bytes 16777216
  278.7 8.4 %copy.35 = bf16[2048,2048]{1,0:T(8,128)(2,1)} copy(bf16[2048,2048]{1,0:T(8,128)(2,1)} %get-tuple-element.18) | data formatting | bytes 16777216
Async XLA Ops:
  0.6 2.9 %copy-start = (bf16[64,2048]{1,0:T(8,128)(2,1)S(1)}, bf16[64,2048]{1,0:T(8,128)(2,1)}, u32[]{:S(2)}) copy-start(bf16[64,2048]{1,0:T(8,128)(2,1)} %param.13) | copy-start | bytes 786436
  0.6 2.9 %copy-start.4 = (bf16[256,64]{0,1:T(8,128)(2,1)S(1)}, bf16[256,64]{0,1:T(8,128)(2,1)}, u32[]{:S(2)}) copy-start(bf16[256,64]{0,1:T(8,128)(2,1)} %param.12) | copy-start | bytes 98308
  2.0 3.1 %copy-start.1 = (bf16[256,2048]{1,0:T(8,128)(2,1)S(1)}, bf16[256,2048]{1,0:T(8,128)(2,1)}, u32[]{:S(2)}) copy-start(bf16[256,2048]{1,0:T(8,128)(2,1)} %param.14) | copy-start | bytes 3145732
  3.6 2.0 copy-start.5
  5.1 3.0 %copy-start.2 = (bf16[2048,256]{1,0:T(8,128)(2,1)S(1)}, bf16[2048,256]{1,0:T(8,128)(2,1)}, u32[]{:S(2)}) copy-start(bf16[2048,256]{1,0:T(8,128)(2,1)} %param.17) | copy-start | bytes 3145732
  5.6 3.1 %copy-start.6 = (bf16[64,256]{1,0:T(8,128)(2,1)S(1)}, bf16[64,256]{1,0:T(8,128)(2,1)}, u32[]{:S(2)}) copy-start(bf16[64,256]{1,0:T(8,128)(2,1)} %param.19) | copy-start | bytes 98308
  8.0 1.0 copy-start.3

commit v2 on v1

--- a/solution.py
+++ b/solution.py
@@ -23,6 +23,7 @@
 LINE = tuple(range(len(PIECES) - 1))
 PAIR = len(PIECES) - 1
 UP, DOWN, SIDE = 0, 1, 2
+STRIP = 128
 
 
 def gather_kernel(
@@ -133,10 +134,7 @@
         send(UP, me, c, c, None, from_own=True)
         send(DOWN, me, c, c, None, from_own=True)
         send(SIDE, me, c, c, None, from_own=True)
-    kept = [pltpu.make_async_copy(own(c), place(me, c), own_sem.at[c]) for c in range(n_pieces)]
-    norm_own = pltpu.make_async_copy(norm, norm_rows(me * widths + w, 1), own_sem.at[n_pieces])
-    for copy in kept:
-        copy.start()
+    norm_own = pltpu.make_async_copy(norm, norm_rows(me * widths + w, 1), own_sem.at[0])
     norm_own.start()
     tile_of = lambda k: norm_copy(norm, me * widths + w, 1, k - 1, k - 1, (me, peers[k - 1]))
     for k in range(1, widths):
@@ -150,6 +148,20 @@
         norm_rows(s * widths, widths), s * widths, widths, side_at, side_at, (partner, w)
     )
     norm_side(me).start()
+
+    wide, tall = gate.shape[1], down.shape[0]
+    columns = pl.ds(pl.multiple_of(me * wide, wide), wide)
+
+    @pl.loop(0, gate.shape[0] // STRIP)
+    def _(i):
+        rows = pl.ds(pl.multiple_of(i * STRIP, STRIP), STRIP)
+        o_gate[rows, columns] = gate[rows, :]
+        o_up[rows, columns] = up[rows, :]
+
+    @pl.loop(0, tall // 16)
+    def _(i):
+        rows = pl.ds(pl.multiple_of(i * 16, 16), 16)
+        o_down[pl.ds(pl.multiple_of(me * tall + i * 16, 16), 16), :] = down[rows, :]
 
     for d in range(1, lines):
         for c in LINE:
@@ -198,8 +210,6 @@
         for c in LINE:
             arrive(partner - d * X, c, z >= d)
             arrive(partner + d * X, c, z + d < lines)
-    for copy in kept:
-        copy.wait()
     for k in range(1, widths):
         tile_of(k).wait_send()
     norm_side(me).wait_send()
@@ -212,25 +222,48 @@
     n_pieces = len(PIECES)
     any_ = pl.BlockSpec(memory_space=pl.ANY)
     vmem = pl.BlockSpec(memory_space=pltpu.VMEM)
-    wide = lambda b: jax.ShapeDtypeStruct((b.shape[0], shards * b.shape[1]), b.dtype)
-    tall = lambda b: jax.ShapeDtypeStruct((shards * b.shape[0], b.shape[1]), b.dtype)
+    wide = lambda b: pltpu.VMEM((b.shape[0], shards * b.shape[1]), b.dtype)
+    tall = lambda b: pltpu.VMEM((shards * b.shape[0], b.shape[1]), b.dtype)
     return pl.pallas_call(
         functools.partial(gather_kernel, shards, widths),
         out_shape=(
             wide(gate), wide(up), tall(down),
-            jax.ShapeDtypeStruct((shards * widths,) + norm.shape[1:], norm.dtype),
+            pltpu.HBM((shards * widths,) + norm.shape[1:], norm.dtype),
         ),
         in_specs=[vmem] * 4,
-        out_specs=(any_,) * 4,
+        out_specs=(vmem,) * 3 + (any_,),
         scratch_shapes=[
             pltpu.SemaphoreType.DMA((3, 2 * lines * n_pieces + lines * X)),
             pltpu.SemaphoreType.DMA((shards * n_pieces,)),
             pltpu.SemaphoreType.DMA((widths + 2 * lines,)),
             pltpu.SemaphoreType.DMA((widths + lines,)),
-            pltpu.SemaphoreType.DMA((n_pieces + 1,)),
+            pltpu.SemaphoreType.DMA((1,)),
         ],
-        compiler_params=pltpu.CompilerParams(collective_id=0, has_side_effects=True),
+        compiler_params=pltpu.CompilerParams(collective_id=0, has_side_effects=True, vmem_limit_bytes=16 * 2**20),
     )(gate, up, down, norm)
+
+
+def write_kernel(gate, up, down, tiles, o_gate, o_up, o_down, o_tiles, sem):
+    pairs = ((gate, o_gate), (up, o_up), (down, o_down))
+    copies = [pltpu.make_async_copy(a, b, sem.at[i]) for i, (a, b) in enumerate(pairs)]
+    for copy in copies:
+        copy.start()
+    o_tiles[...] = tiles[...]
+    for copy in copies:
+        copy.wait()
+
+
+def write_out(gate, up, down, tiles):
+    any_ = pl.BlockSpec(memory_space=pl.ANY)
+    vmem = pl.BlockSpec(memory_space=pltpu.VMEM)
+    return pl.pallas_call(
+        write_kernel,
+        out_shape=tuple(jax.ShapeDtypeStruct(a.shape, a.dtype) for a in (gate, up, down, tiles)),
+        in_specs=[any_] * 3 + [vmem],
+        out_specs=(any_,) * 3 + (vmem,),
+        scratch_shapes=[pltpu.SemaphoreType.DMA((3,))],
+        compiler_params=pltpu.CompilerParams(vmem_limit_bytes=4 * 2**20),
+    )(gate, up, down, tiles)
 
 
 def body(
@@ -252,7 +285,7 @@
     up = merged(w_up, low_up, high_up)
     down = merged(w_down, low_down, high_down)
     gain = norm_train + norm_step
-    if shards % X or gate.shape[0] % 128 or down.shape[0] % 256 or gain.shape[0] > 128:
+    if shards % X or gate.shape[0] % 128 or down.shape[0] % 256 or gate.shape[0] % STRIP or gain.shape[0] > 128:
         gate, up, down = (
             lax.all_gather(gate, "shard", axis=0, tiled=True),
             lax.all_gather(up, "shard", axis=0, tiled=True),
@@ -263,6 +296,7 @@
     count = gain.shape[0]
     tile = jnp.pad(gain.reshape(1, 1, count), ((0, 0), (0, 7), (0, 128 - count)))
     gate, up, down, tiles = gather_all(shards, widths, gate.T, up.T, down.T, tile)
+    gate, up, down, tiles = write_out(gate, up, down, tiles)
     return gate, up, down, tiles[:, 0, :count].reshape(-1).astype(jnp.bfloat16)
 
 

time: 287 us -> 267 us (0.930)
  local copies, waits for them, and re-layouts: 30.6 us -> 6.1 us
  Pallas kernels: 250 us -> 256 us
    unnamed x20 -> x13, local copies, waits for them, and re-layouts: 28.4 us -> 5.37 us
    pallas_call x0 -> x1, Pallas kernels: none -> 8.7 us  [write_out(): pl.pallas_call(write_kernel, out_shape=tuple((jax.ShapeDtypeStruct(a.shap...]
where the time goes in v2:
time: 267 us
  Pallas kernels  256 us (96%)
  local copies, waits for them, and re-layouts  6.1 us (2%)
  matrix products  3.38 us (1%)
    pallas_call x1, Pallas kernels, gather_all(): pl.pallas_call(functools.partial(gather_kernel, shards, widths), out_shap...  247 us
    pallas_call x1, Pallas kernels, write_out(): pl.pallas_call(write_kernel, out_shape=tuple((jax.ShapeDtypeStruct(a.shap...  8.7 us
    unnamed x13, local copies, waits for them, and re-layouts  5.37 us

profile of v2, /device:TPU:0, one launch (start us, length us, event | category | flops | bytes accessed | tf_op | source)
XLA Modules:
  0.0 267.1 jit_solution(270420570686985209)
XLA Ops:
  0.6 0.0 copy-start
  0.6 0.0 copy-start.2
  0.7 0.7 add_bitcast_fusion
  1.4 1.5 copy.21
  2.9 0.0 copy-done
  2.9 0.0 copy-done.2
  2.9 0.0 copy-start.3
  2.9 0.5 fusion.8.gate
  3.4 1.5 copy.23
  4.9 0.0 copy-done.3
  4.9 0.0 copy-start.4
  4.9 1.5 fusion.7.up
  6.4 1.5 copy.25
  7.9 0.0 copy-done.4
  7.9 1.4 fusion.6.down
  9.3 247.4 %shard_map.138 = (bf16[2048,2048]{1,0:T(8,128)(2,1)S(1)}, bf16[2048,2048]{1,0:T(8,128)(2,1)S(1)}, bf16[2048,2048]{1,0:T(8,128)(2,1)S(1)}, f32[32,8,128]{2,1,0:T(8,128)}) custom-call(bf16[2048,256]{1,0:T(8,128)(2,1)S(1)} %fusion.8.gate, bf16[2048,256]{1,0:T(8,128)(2,1)S(1)} %fusion.7.up, bf16[256,2048]{1,0:T(8,128)(2,1)S(1)} %fusion.6.down, ...), custom_call_target="tpu_custom_call" | custom-call | tf_op jit(solution)/shard_map/pallas_call | solution.py:227
  256.8 0.0 copy-start.1
  256.8 0.9 copy-done.1
  257.7 8.7 %shard_map.139 = (bf16[2048,2048]{1,0:T(8,128)(2,1)}, bf16[2048,2048]{1,0:T(8,128)(2,1)}, bf16[2048,2048]{1,0:T(8,128)(2,1)}, f32[32,8,128]{2,1,0:T(8,128)S(1)}) custom-call(bf16[2048,2048]{1,0:T(8,128)(2,1)S(1)} %get-tuple-element.12.gate, bf16[2048,2048]{1,0:T(8,128)(2,1)S(1)} %get-tuple-element.13.up, bf16[2048,2048]{1,0:T(8,128)(2,1)S(1)} %get-tuple-element.14.down, ...), custom_call_target="tpu_custom_call" | custom-call | tf_op jit(solution)/shard_map/pallas_call | solution.py:259
  266.4 0.1 fusion.9
  266.4 0.7 convert_element_type.30
  (1 shorter events, 0.0 us)
Async XLA Ops:
  0.6 2.2 copy-start
  0.6 2.2 copy-start.2
  2.9 2.0 copy-start.3
  4.9 3.0 %copy-start.4 = (bf16[64,256]{1,0:T(8,128)(2,1)S(1)}, bf16[64,256]{1,0:T(8,128)(2,1)}, u32[]{:S(2)}) copy-start(bf16[64,256]{1,0:T(8,128)(2,1)} %param.19) | copy-start | bytes 98308
  256.8 0.9 copy-start.1

commit v3 on v2

--- a/solution.py
+++ b/solution.py
@@ -266,6 +266,48 @@
     )(gate, up, down, tiles)
 
 
+def merge_kernel(*refs):
+    ins, outs = refs[:9], refs[9:]
+    for t in range(3):
+        w, low, high = ins[3 * t : 3 * t + 3]
+        delta = lax.dot_general(
+            high[...], low[...], (((0,), (0,)), ((), ())), preferred_element_type=jnp.float32
+        )
+        outs[t][...] = (w[...].astype(jnp.float32).T + mix_rate * delta).astype(jnp.bfloat16)
+
+
+def merge_all(strip, *arrays):
+    wg, lg, hg, wu, lu, hu, wd, ld, hd = arrays
+    rank = lg.shape[1]
+
+    def first(w):
+        tall = w.shape[0]
+        return [
+            pl.BlockSpec((tall, strip), lambda i: (0, i)),
+            pl.BlockSpec((rank, tall), lambda i: (0, 0)),
+            pl.BlockSpec((rank, strip), lambda i: (0, i)),
+        ]
+
+    wide = wd.shape[1]
+    last = [
+        pl.BlockSpec((strip, wide), lambda i: (i, 0)),
+        pl.BlockSpec((rank, strip), lambda i: (0, i)),
+        pl.BlockSpec((rank, wide), lambda i: (0, 0)),
+    ]
+    return pl.pallas_call(
+        merge_kernel,
+        grid=(wg.shape[1] // strip,),
+        out_shape=tuple(jax.ShapeDtypeStruct(w.shape[::-1], w.dtype) for w in (wg, wu, wd)),
+        in_specs=first(wg) + first(wu) + last,
+        out_specs=(
+            pl.BlockSpec((strip, wg.shape[0]), lambda i: (i, 0)),
+            pl.BlockSpec((strip, wu.shape[0]), lambda i: (i, 0)),
+            pl.BlockSpec((wide, strip), lambda i: (0, i)),
+        ),
+        compiler_params=pltpu.CompilerParams(vmem_limit_bytes=16 * 2**20),
+    )(wg, lg.T, hg, wu, lu.T, hu, wd, ld.T, hd)
+
+
 def body(
     shards,
     widths,
@@ -285,7 +327,7 @@
     up = merged(w_up, low_up, high_up)
     down = merged(w_down, low_down, high_down)
     gain = norm_train + norm_step
-    if shards % X or gate.shape[0] % 128 or down.shape[0] % 256 or gate.shape[0] % STRIP or gain.shape[0] > 128:
+    if shards % X or gate.shape[0] % 128 or down.shape[0] % 256 or gate.shape[1] % 256 or down.shape[0] != gate.shape[1] or gain.shape[0] > 128:
         gate, up, down = (
             lax.all_gather(gate, "shard", axis=0, tiled=True),
             lax.all_gather(up, "shard", axis=0, tiled=True),
@@ -295,7 +337,10 @@
         return gate.T, up.T, down.T, gain
     count = gain.shape[0]
     tile = jnp.pad(gain.reshape(1, 1, count), ((0, 0), (0, 7), (0, 128 - count)))
-    gate, up, down, tiles = gather_all(shards, widths, gate.T, up.T, down.T, tile)
+    gate, up, down = merge_all(
+        256, w_gate, low_gate, high_gate, w_up, low_up, high_up, w_down, low_down, high_down
+    )
+    gate, up, down, tiles = gather_all(shards, widths, gate, up, down, tile)
     gate, up, down, tiles = write_out(gate, up, down, tiles)
     return gate, up, down, tiles[:, 0, :count].reshape(-1).astype(jnp.bfloat16)
 

time: 267 us -> 272 us (1.019)
  local copies, waits for them, and re-layouts: 6.1 us -> 10.4 us
  Pallas kernels: 256 us -> 260 us
  matrix products: 3.38 us -> 0 us
    unnamed x13 -> x20, local copies, waits for them, and re-layouts: 5.37 us -> 9.69 us
    dot_general x3 -> x0, matrix products: 3.38 us -> none  [merged(): jnp.dot(low, high, preferred_element_type=jnp.float32)]
    pallas_call x0 -> x1, Pallas kernels: none -> 3.38 us  [merge_all(): pl.pallas_call(merge_kernel, grid=(wg.shape[1] // strip,), out_shape=tupl...]
where the time goes in v3:
time: 272 us; the launch traced here: 271 us
  Pallas kernels  260 us (96%)
  local copies, waits for them, and re-layouts  10.4 us (4%)
    pallas_call x1, Pallas kernels, gather_all(): pl.pallas_call(functools.partial(gather_kernel, shards, widths), out_shap...  247 us
    unnamed x20, local copies, waits for them, and re-layouts  9.69 us
    pallas_call x1, Pallas kernels, write_out(): pl.pallas_call(write_kernel, out_shape=tuple((jax.ShapeDtypeStruct(a.shap...  8.7 us

profile of v3, /device:TPU:0, one launch (start us, length us, event | category | flops | bytes accessed | tf_op | source)
XLA Modules:
  0.0 271.3 jit_solution(9986282400698138273)
XLA Ops:
  0.6 0.7 add_bitcast_fusion
  1.3 0.0 copy-start
  1.3 1.2 copy-done
  2.5 0.0 copy-start.1
  2.5 1.2 copy-done.1
  3.8 0.0 copy-start.2
  3.8 1.2 copy-done.2
  5.0 0.0 copy-start.3
  5.0 0.9 copy-done.3
  5.9 0.0 copy-start.4
  5.9 0.9 copy-done.4
  6.9 0.0 copy-start.5
  6.9 0.9 copy-done.5
  7.8 0.0 copy-start.7
  7.8 0.8 copy-done.7
  8.6 0.0 copy-start.8
  8.6 0.8 copy-done.8
  9.4 0.0 copy-start.9
  9.4 0.8 copy-done.9
  10.1 3.4 %shard_map.138 = (bf16[2048,256]{1,0:T(8,128)(2,1)S(1)}, bf16[2048,256]{1,0:T(8,128)(2,1)S(1)}, bf16[256,2048]{1,0:T(8,128)(2,1)S(1)}) custom-call(bf16[256,2048]{1,0:T(8,128)(2,1)S(1)} %copy-done, bf16[64,256]{1,0:T(8,128)(2,1)S(1)} %bitcast.6, bf16[64,2048]{1,0:T(8,128)(2,1)S(1)} %copy-done.3, bf16[256,2048]{1,0:T(8,128)(2,1)S(1)} %copy-done.1, ...), custom_call_target="tpu_custom_call" | custom-call | tf_op jit(solution)/shard_map/pallas_call | solution.py:297
  13.5 247.5 %shard_map.139 = (bf16[2048,2048]{1,0:T(8,128)(2,1)S(1)}, bf16[2048,2048]{1,0:T(8,128)(2,1)S(1)}, bf16[2048,2048]{1,0:T(8,128)(2,1)S(1)}, f32[32,8,128]{2,1,0:T(8,128)}) custom-call(bf16[2048,256]{1,0:T(8,128)(2,1)S(1)} %get-tuple-element.15.gate, bf16[2048,256]{1,0:T(8,128)(2,1)S(1)} %get-tuple-element.16.up, bf16[256,2048]{1,0:T(8,128)(2,1)S(1)} %get-tuple-element.17.down, ...), custom_call_target="tpu_custom_call" | custom-call | tf_op jit(solution)/shard_map/pallas_call | solution.py:227
  261.0 0.0 copy-start.6
  261.0 0.9 copy-done.6
  261.9 8.7 %shard_map.140 = (bf16[2048,2048]{1,0:T(8,128)(2,1)}, bf16[2048,2048]{1,0:T(8,128)(2,1)}, bf16[2048,2048]{1,0:T(8,128)(2,1)}, f32[32,8,128]{2,1,0:T(8,128)S(1)}) custom-call(bf16[2048,2048]{1,0:T(8,128)(2,1)S(1)} %get-tuple-element.18.gate, bf16[2048,2048]{1,0:T(8,128)(2,1)S(1)} %get-tuple-element.19.up, bf16[2048,2048]{1,0:T(8,128)(2,1)S(1)} %get-tuple-element.20.down, ...), custom_call_target="tpu_custom_call" | custom-call | tf_op jit(solution)/shard_map/pallas_call | solution.py:259
  270.6 0.1 fusion
  270.6 0.7 convert_element_type.6
  (1 shorter events, 0.0 us)
Async XLA Ops:
  1.3 1.2 copy-start
  2.5 1.2 copy-start.1
  3.8 1.2 copy-start.2
  5.0 0.9 copy-start.3
  5.9 0.9 copy-start.4
  6.9 0.9 copy-start.5
  7.8 0.8 copy-start.7
  8.6 0.8 copy-start.8
  9.4 0.8 copy-start.9
  261.0 0.9 copy-start.6
